TPU v7x, 32 devices: a whole 2x2x4 slice. The times are simulated.
32 devices in a mesh: dp: 2 (over y), row: 4 (over x, core), col: 4 (over z).
Axes of the slice: x: 2, y: 2, z: 4, core: 2. Of those that a mesh axis runs over, the one named last changes fastest.
Arguments:
- tokens: bfloat16 [2048, 8192], P(('dp', 'col'), 'row'), may hold values from -6 to 6
- frozen_weight: bfloat16 [8192, 8192], P('row', 'col'), may hold values from -0.0625 to 0.0625
- input_adapter_factor: bfloat16 [16, 8192], P(None, 'row'), may hold values from -0.0625 to 0.0625
- output_adapter_factor: bfloat16 [16, 8192], P(None, 'col'), may hold values from -1.5 to 1.5
- magnitude: float32 [8192], P('col'), may hold values from 0.5 to 2
- cotangent: bfloat16 [2048, 8192], P(('dp', 'row'), 'col'), may hold values from -6 to 6
- sequence_lengths: int32 [2, 8], P('dp'), may hold values from 1 to 512, 1024 in all within a row
Outputs:
- projected: bfloat16 [2048, 8192], P(('dp', 'row'), 'col')
- grad_mag: float32 [8192], P('col')
- input_factor_gradient: float32 [16, 8192], P(None, 'row')
- grad_b: float32 [16, 8192], P(None, 'col')
Inputs may be any that keep to these rules, and one draw needn't show every extreme that they name: `sequence_lengths`: each group's 8 lengths sum to 1024, and one of them is exactly 512.
All inputs are finite; a program needn't handle non-finite values.
Results may differ from a plain program's by a relative error of at most 0.0052.
Values may be sent and summed in bfloat16 or wider, within the bound.
No kernel may reach another device: no remote copies, remote signals or barrier semaphores. Data moves between devices by JAX's collectives and lax.ppermute only.
A program may use at most 64 MiB of HBM per device.

v0:
```python
import jax
import jax.numpy as jnp
from jax import lax
from jax.sharding import PartitionSpec as P

norm_eps = 1e-06
highest_precision = lax.Precision.HIGHEST


def contract_product(left, right, left_dim, right_dim):
    return lax.dot_general(
        left, right, (((left_dim,), (right_dim,)), ((), ())), preferred_element_type=jnp.float32
    )


def per_device(
    tokens,
    frozen_weight,
    input_adapter_factor,
    output_adapter_factor,
    magnitude,
    cotangent,
    sequence_lengths,
):
    row_count = lax.axis_size("row")
    col_count = lax.axis_size("col")
    row_index = lax.axis_index("row")
    col_index = lax.axis_index("col")
    group_index = lax.axis_index("dp")
    local_rows = tokens.shape[0]
    group_rows = local_rows * col_count
    block_rows = group_rows // row_count
    adapter_rank_size = input_adapter_factor.shape[0]
    low_rank_update = contract_product(input_adapter_factor, output_adapter_factor, 0, 0)
    merged = frozen_weight.astype(jnp.float32) + low_rank_update
    norm_terms = jnp.sum(merged * merged, axis=0)
    gram_partial_terms = contract_product(input_adapter_factor, input_adapter_factor, 1, 1)
    merged_factor_terms = jnp.dot(
        input_adapter_factor, frozen_weight, preferred_element_type=jnp.float32
    ) + jnp.dot(
        gram_partial_terms, output_adapter_factor.astype(jnp.float32), precision=highest_precision
    )
    portion = lax.all_gather(tokens, "col", axis=0, tiled=True)
    base_piece = jnp.dot(portion, frozen_weight, preferred_element_type=jnp.float32)
    down_portion = contract_product(portion, input_adapter_factor, 1, 1)
    frozen_rows, down_rows = (
        lax.psum_scatter(base_piece, "row", scatter_dimension=0, tiled=True),
        lax.psum_scatter(down_portion, "row", scatter_dimension=0, tiled=True),
    )
    norm_sq, merged_input_factor = lax.psum((norm_terms, merged_factor_terms), "row")
    down_activations = down_rows.astype(jnp.bfloat16)
    col_norm = jnp.sqrt(norm_sq + norm_eps)
    col_scale = magnitude / col_norm
    query_projection = frozen_rows + jnp.dot(
        down_activations, output_adapter_factor, preferred_element_type=jnp.float32
    )
    projected = (query_projection * col_scale[None, :]).astype(jnp.bfloat16)
    lengths = sequence_lengths[0]
    ends = jnp.cumsum(lengths, dtype=jnp.int32)
    starts = ends - lengths
    positions = row_index * block_rows + jnp.arange(block_rows, dtype=jnp.int32)
    inside = (positions[:, None] >= starts[None, :]) & (positions[:, None] < ends[None, :])
    inverse = 1.0 / lengths.astype(jnp.float32)
    weights = jnp.sum(jnp.where(inside, inverse[None, :], jnp.float32(0.0)), axis=1)
    grad_out = cotangent.astype(jnp.float32) * weights[:, None]
    scale_terms = jnp.sum(grad_out * query_projection, axis=0)
    projection_gradient = (grad_out * col_scale[None, :]).astype(jnp.bfloat16)
    bgrad_terms = contract_product(down_activations, projection_gradient, 0, 0)
    scale_grad, bgrad_data = lax.psum((scale_terms, bgrad_terms), ("dp", "row"))
    grad_mag = scale_grad / col_norm
    norm_coefficient = -scale_grad * magnitude / (col_norm * col_norm * col_norm)
    grad_b = bgrad_data + merged_input_factor * norm_coefficient[None, :]
    backward_terms = contract_product(projection_gradient, output_adapter_factor, 1, 1)
    padded = lax.dynamic_update_slice_in_dim(
        jnp.zeros((group_rows, adapter_rank_size), jnp.float32),
        backward_terms,
        row_index * block_rows,
        0,
    )
    backward_rows = lax.psum(padded, ("row", "col")).astype(jnp.bfloat16)
    back_mine = lax.dynamic_slice_in_dim(backward_rows, col_index * local_rows, local_rows, 0)
    row_term = contract_product(back_mine, tokens, 0, 0)
    scaled_output_factor = (
        output_adapter_factor.astype(jnp.float32) * norm_coefficient[None, :]
    ).astype(jnp.bfloat16)
    norm_term = contract_product(scaled_output_factor, frozen_weight, 1, 1) + jnp.dot(
        contract_product(scaled_output_factor, output_adapter_factor, 1, 1),
        input_adapter_factor.astype(jnp.float32),
        precision=highest_precision,
    )
    first_group = (group_index == 0).astype(jnp.float32)
    input_factor_gradient = lax.psum(row_term + first_group * norm_term, ("dp", "col"))
    return (projected, grad_mag, input_factor_gradient, grad_b)


def solution(mesh):
    in_specs = (
        P(("dp", "col"), "row"),
        P("row", "col"),
        P(None, "row"),
        P(None, "col"),
        P("col"),
        P(("dp", "row"), "col"),
        P("dp", None),
    )
    out_specs = (P(("dp", "row"), "col"), P("col"), P(None, "row"), P(None, "col"))
    return jax.shard_map(
        per_device, mesh=mesh, in_specs=in_specs, out_specs=out_specs, check_vma=False
    )
```

profile of v0, /device:TPU:0, one launch (start us, length us, event | category | flops | bytes accessed | tf_op | source)
XLA Modules:
  0.0 366.2 jit_solution(13270679273868545477)
XLA Ops:
  7.2 0.0 all-gather.2.cloned.1.call-start
  7.2 0.7 all-gather.2.cloned.1.call-update
  7.9 0.0 reduce-scatter.5.cloned.1.call-start
  8.0 85.1 %all-gather.2.cloned.1.call-done = bf16[1024,2048]{1,0:T(8,128)(2,1)} async-done(((bf16[256,2048]{1,0:T(8,128)(2,1)}), bf16[1024,2048]{1,0:T(8,128)(2,1)}) %all-gather.2.cloned.1.call-update) | async-done | bytes 4194320 | tf_op jit(solution)/shard_map/all_gather | solution.py:43
  93.1 4.0 %fusion.14 = f32[1024,16]{0,1:T(8,128)} fusion(bf16[1024,2048]{1,0:T(8,128)(2,1)} %all-gather.2.cloned.1.call-done, bf16[16,2048]{1,0:T(8,128)(2,1)S(1)} %copy-done), kind=kOutput, calls=%fused_computation.33 | convolution fusion | flops 67108864 | bytes 4325376 | tf_op jit(solution)/shard_map/dot_general | solution.py:11
  97.1 0.0 reduce-scatter.3.cloned.1.call-start
  97.1 14.4 %fusion.13 = f32[1024,2048]{1,0:T(8,128)} fusion(bf16[1024,2048]{1,0:T(8,128)(2,1)} %all-gather.2.cloned.1.call-done, bf16[2048,2048]{1,0:T(8,128)(2,1)} %param.8), kind=kOutput, calls=%fused_computation.32 | convolution fusion | flops 8589934592 | bytes 20971520 | tf_op jit(solution)/shard_map/dot_general | solution.py:44
  111.6 0.0 all-reduce.8.cloned.1.call-start
  111.6 0.1 fusion.16
  111.8 4.6 %fusion.15 = f32[16,2048]{1,0:T(8,128)S(1)} fusion(bf16[16,2048]{1,0:T(8,128)(2,1)S(1)} %copy-done, bf16[2048,2048]{1,0:T(8,128)(2,1)} %param.8), kind=kOutput, calls=%fused_computation.34 | convolution fusion | flops 134217728 | bytes 8585216 | tf_op jit(solution)/shard_map/dot_general | solution.py:38
  116.4 0.9 convolution_add_fusion.1
  117.3 0.0 all-reduce.6.cloned.1.call-start
  117.4 5.9 %multiply_reduce_fusion = f32[2048]{0:T(1024)S(1)} fusion(bf16[2048,2048]{1,0:T(8,128)(2,1)} %param.8, bf16[16,2048]{1,0:T(8,128)(2,1)S(1)} %copy-done, bf16[16,2048]{1,0:T(8,128)(2,1)S(1)} %copy-done.2), kind=kOutput, calls=%fused_computation | convolution fusion | flops 150992896 | bytes 8527872 | tf_op jit(solution)/shard_map/dot_general | solution.py:11
  123.3 0.2 reduce-window.4
  123.5 6.5 %psum.42 = f32[2048]{0:T(1024)S(1)} all-reduce(f32[2048]{0:T(1024)S(1)} %multiply_reduce_fusion), channel_id=1, replica_groups=mesh['dp'=2,'row'=4,'col'=4] {'row'}, use_global_device_ids=true, to_apply=%region_3.0 | all-reduce | flops 2048 | bytes 16384 | tf_op jit(solution)/shard_map/psum | solution.py:50
  130.1 0.1 select_reduce_fusion
  130.2 0.5 convolution_dynamic-update-slice_fusion
  130.7 69.2 %psum.44 = bf16[1024,16]{1,0:T(8,128)(2,1)S(1)} all-reduce(f32[1024,16]{1,0:T(8,128)S(1)} %convolution_dynamic-update-slice_fusion), channel_id=1, replica_groups=mesh['dp'=2,'row'=4,'col'=4] {'row','col'}, use_global_device_ids=true, to_apply=%region_8.9 | all-reduce | flops 16384 | bytes 98304 | tf_op jit(solution)/shard_map/psum | solution.py:80
  200.0 1.8 fusion.1
  201.8 0.0 all-reduce.4.cloned.1.call-start
  201.9 3.2 multiply_reduce_fusion.1
  205.1 12.1 %psum.43 = f32[2048]{0:T(1024)S(1)} all-reduce(f32[2048]{0:T(1024)S(1)} %get-tuple-element.4), channel_id=1, replica_groups=mesh['dp'=2,'row'=4,'col'=4] {'dp','row'}, use_global_device_ids=true, to_apply=%region_7.8 | all-reduce | flops 2048 | bytes 16384 | tf_op jit(solution)/shard_map/psum | solution.py:69
  217.1 0.6 fusion.6
  217.8 5.7 %fusion.3 = f32[16,2048]{1,0:T(8,128)S(1)} fusion(bf16[2048,2048]{1,0:T(8,128)(2,1)} %param.8, bf16[16,2048]{1,0:T(8,128)(2,1)S(1)} %copy-done.2, f32[2048]{0:T(1024)S(1)} %get-tuple-element.6), kind=kOutput, calls=%fused_computation.16 | convolution fusion | flops 134316032 | bytes 8593408 | tf_op jit(solution)/shard_map/dot_general | solution.py:11
  223.5 0.1 fusion.2
  223.6 0.2 fusion
  223.9 0.9 convolution_add_fusion.3
  224.8 2.4 all-reduce.8.cloned.1.call-done
  227.2 57.0 %all-reduce.6.cloned.1.call-done = f32[16,2048]{1,0:T(8,128)} async-done(((f32[16,2048]{1,0:T(8,128)}), f32[16,2048]{1,0:T(8,128)}) %all-reduce.6.cloned.1.call-update) | async-done | bytes 131088 | tf_op jit(solution)/shard_map/psum | solution.py:69
  284.2 1.6 multiply_add_fusion
  285.9 71.9 %all-reduce.4.cloned.1.call-done = f32[16,2048]{1,0:T(8,128)} async-done(((f32[16,2048]{1,0:T(8,128)}), f32[16,2048]{1,0:T(8,128)}) %all-reduce.4.cloned.1.call-update) | async-done | bytes 131088 | tf_op jit(solution)/shard_map/psum | solution.py:92
  357.8 1.6 copy.15
  (24 shorter events, 0.2 us)
Async XLA Ops:
  7.2 85.9 %copy-start = (bf16[16,2048]{1,0:T(8,128)(2,1)S(1)}, bf16[16,2048]{1,0:T(8,128)(2,1)}, u32[]{:S(2)}) copy-start(bf16[16,2048]{1,0:T(8,128)(2,1)} %param.9) | copy-start | bytes 196612
  7.2 85.9 %all-gather.2.cloned.1.call-start = ((), (), s32[]{:S(2)}) async-start(), calls=%async_computation.2 | async-start | bytes 5242880 | tf_op jit(solution)/shard_map/all_gather | solution.py:43
  7.9 192.0 %reduce-scatter.5.cloned.1.call-start = ((), (), s32[]{:S(2)}) async-start(), calls=%async_computation.4 | async-start | bytes 81920 | tf_op jit(solution)/shard_map/reduce_scatter | solution.py:48
  97.1 104.8 %reduce-scatter.3.cloned.1.call-start = ((), (), s32[]{:S(2)}) async-start(), calls=%async_computation.3 | async-start | bytes 10485760 | tf_op jit(solution)/shard_map/reduce_scatter | solution.py:47
  111.6 115.7 %all-reduce.8.cloned.1.call-start = ((), (), s32[]{:S(2)}) async-start(), calls=%async_computation.7 | async-start | bytes 262144 | tf_op jit(solution)/shard_map/psum | solution.py:50
  111.8 4.6 %copy-start.2 = (bf16[16,2048]{1,0:T(8,128)(2,1)S(1)}, bf16[16,2048]{1,0:T(8,128)(2,1)}, u32[]{:S(2)}) copy-start(bf16[16,2048]{1,0:T(8,128)(2,1)} %param.10) | copy-start | bytes 196612
  117.3 166.9 %all-reduce.6.cloned.1.call-start = ((), (), s32[]{:S(2)}) async-start(), calls=%async_computation.6 | async-start | bytes 262144 | tf_op jit(solution)/shard_map/psum | solution.py:69
  117.3 5.9 %copy-start.5 = (s32[1,8]{1,0:T(1,128)S(1)}, s32[1,8]{1,0:T(1,128)}, u32[]{:S(2)}) copy-start(s32[1,8]{1,0:T(1,128)} %param.13) | copy-start | bytes 100
  117.4 12.7 %copy-start.4 = (f32[2048]{0:T(1024)S(1)}, f32[2048]{0:T(1024)}, u32[]{:S(2)}) copy-start(f32[2048]{0:T(1024)} %param.11) | copy-start | bytes 24580
  117.4 12.8 %copy-start.3 = (bf16[256,2048]{1,0:T(8,128)(2,1)S(1)}, bf16[256,2048]{1,0:T(8,128)(2,1)}, u32[]{:S(2)}) copy-start(bf16[256,2048]{1,0:T(8,128)(2,1)} %param.12) | copy-start | bytes 3145732
  201.8 156.0 %all-reduce.4.cloned.1.call-start = ((), (), s32[]{:S(2)}) async-start(), calls=%async_computation.5 | async-start | bytes 262144 | tf_op jit(solution)/shard_map/psum | solution.py:92
  217.8 6.1 %copy-start.1 = (bf16[256,2048]{1,0:T(8,128)(2,1)S(1)}, bf16[256,2048]{1,0:T(8,128)(2,1)}, u32[]{:S(2)}) copy-start(bf16[256,2048]{1,0:T(8,128)(2,1)} %param.7) | copy-start | bytes 3145732
Sparse Core Ops, SparseCore 0:
  9.6 83.4 all-gather.1
  97.2 18.0 reduce-scatter.4
  117.9 75.6 reduce-scatter.2
  195.8 31.4 all-reduce.7
  230.7 53.4 all-reduce.5
  288.0 69.7 all-reduce.3
where the time goes:
time: 367 us; the launch traced here: 366 us
  waiting for transfers between devices  217 us (59%)
  blocking collectives  87.8 us (24%)
  matrix products  42.5 us (12%)
  between operations  14.3 us (4%)
    all_gather x1, waiting for transfers between devices, per_device(): portion = lax.all_gather(tokens, 'col', axis=0, tiled=True)  85.1 us
    psum x1, waiting for transfers between devices, per_device(): lax.psum(row_term + first_group * norm_term, ('dp', 'col'))  71.9 us
    psum x1, blocking collectives, per_device(): backward_rows = lax.psum(padded, ('row', 'col')).astype(jnp.bfloat16)  69.2 us
    psum x1, waiting for transfers between devices, per_device(): scale_grad, bgrad_data = lax.psum((scale_terms, bgrad_terms), ('dp', 'row'))  57 us
    dot_general x8, matrix products, contract_product(): lax.dot_general(left, right, (((left_dim,), (right_dim,)), ((), ())), pre...  19.1 us
    dot_general x1, matrix products, per_device(): jnp.dot(portion, frozen_weight, preferred_element_type=jnp.float32)  14.4 us
    psum x1, blocking collectives, per_device(): scale_grad, bgrad_data = lax.psum((scale_terms, bgrad_terms), ('dp', 'row'))  12.1 us
  transfers between devices with their start and end apart: 6, of which 4 were waited for; matrix products, arithmetic and copies ran while one was open for 11% of the time, Pallas kernels for 0%

commit v1 on v0

--- a/solution.py
+++ b/solution.py
@@ -22,6 +22,10 @@
     cotangent,
     sequence_lengths,
 ):
+
+    def see_page(my_tile, row_axis):
+        return jnp.sum(jax.lax.all_gather(my_tile, axis_name=row_axis), 0)
+
     row_count = lax.axis_size("row")
     col_count = lax.axis_size("col")
     row_index = lax.axis_index("row")
@@ -77,7 +81,7 @@
         row_index * block_rows,
         0,
     )
-    backward_rows = lax.psum(padded, ("row", "col")).astype(jnp.bfloat16)
+    backward_rows = see_page(padded, ("row", "col")).astype(jnp.bfloat16)
     back_mine = lax.dynamic_slice_in_dim(backward_rows, col_index * local_rows, local_rows, 0)
     row_term = contract_product(back_mine, tokens, 0, 0)
     scaled_output_factor = (

time: 367 us -> 401 us (1.093)
  waiting for transfers between devices: 217 us -> 316 us
  blocking collectives: 87.8 us -> 21.3 us
    reduce_scatter x1, waiting for transfers between devices: 0.02 us -> 72 us  [per_device(): lax.psum_scatter(base_piece, 'row', scatter_dimension=0, tiled=True)]
    psum x1 -> x0, blocking collectives: 69.2 us -> none  [per_device(): backward_rows = lax.psum(padded, ('row', 'col')).astype(jnp.bfloat16)]
    reduce_scatter x1, waiting for transfers between devices: 0.02 us -> 20.3 us  [per_device(): lax.psum_scatter(down_portion, 'row', scatter_dimension=0, tiled=True)]
    all_gather x1, waiting for transfers between devices: 85.1 us -> 68.4 us  [per_device(): portion = lax.all_gather(tokens, 'col', axis=0, tiled=True)]
    all_gather x0 -> x1, waiting for transfers between devices: none -> 14.9 us  [see_page(): return jnp.sum(jax.lax.all_gather(my_tile, axis_name=row_axis), 0)]
    psum x1, waiting for transfers between devices: 2.4 us -> 10.3 us  [per_device(): lax.psum((norm_terms, merged_factor_terms), 'row')]
  transfers between devices with their start and end apart: 6 -> 7, of which waited for: 4 -> 7; matrix products, arithmetic and copies ran while one was open for 11% -> 12% of each run, Pallas kernels for 0% -> 0%
where the time goes in v1:
time: 401 us
  waiting for transfers between devices  316 us (79%)
  matrix products  42.4 us (11%)
  blocking collectives  21.3 us (5%)
  between operations  14.3 us (4%)
  other arithmetic  4.48 us (1%)
    psum x1, waiting for transfers between devices, per_device(): lax.psum(row_term + first_group * norm_term, ('dp', 'col'))  72.1 us
    reduce_scatter x1, waiting for transfers between devices, per_device(): lax.psum_scatter(base_piece, 'row', scatter_dimension=0, tiled=True)  72 us
    all_gather x1, waiting for transfers between devices, per_device(): portion = lax.all_gather(tokens, 'col', axis=0, tiled=True)  68.4 us
    psum x1, waiting for transfers between devices, per_device(): scale_grad, bgrad_data = lax.psum((scale_terms, bgrad_terms), ('dp', 'row'))  57 us
    reduce_scatter x1, waiting for transfers between devices, per_device(): lax.psum_scatter(down_portion, 'row', scatter_dimension=0, tiled=True)  20.3 us
    dot_general x8, matrix products, contract_product(): lax.dot_general(left, right, (((left_dim,), (right_dim,)), ((), ())), pre...  19.1 us
    all_gather x1, waiting for transfers between devices, see_page(): return jnp.sum(jax.lax.all_gather(my_tile, axis_name=row_axis), 0)  14.9 us
    dot_general x1, matrix products, per_device(): jnp.dot(portion, frozen_weight, preferred_element_type=jnp.float32)  14.4 us
  transfers between devices with their start and end apart: 7, of which 7 were waited for; matrix products, arithmetic and copies ran while one was open for 12% of the time, Pallas kernels for 0%

profile of v1, /device:TPU:0, one launch (start us, length us, event | category | flops | bytes accessed | tf_op | source)
XLA Modules:
  0.0 400.8 jit_solution(7943701640903856582)
XLA Ops:
  7.2 0.7 all-gather.3.cloned.1.call-update
  8.0 0.8 reduce-window.4
  8.8 5.9 %multiply_reduce_fusion = f32[2048]{0:T(1024)S(1)} fusion(bf16[2048,2048]{1,0:T(8,128)(2,1)} %param.8, bf16[16,2048]{1,0:T(8,128)(2,1)S(1)} %copy-done, bf16[16,2048]{1,0:T(8,128)(2,1)} %param.10), kind=kOutput, calls=%fused_computation | convolution fusion | flops 150992896 | bytes 8527872 | tf_op jit(solution)/shard_map/dot_general | solution.py:11
  14.7 8.5 %psum.35 = f32[2048]{0:T(1024)S(1)} all-reduce(f32[2048]{0:T(1024)S(1)} %multiply_reduce_fusion), channel_id=1, replica_groups=mesh['dp'=2,'row'=4,'col'=4] {'row'}, use_global_device_ids=true, to_apply=%region_3.0 | all-reduce | flops 2048 | bytes 16384 | tf_op jit(solution)/shard_map/psum | solution.py:54
  23.3 0.1 select_reduce_fusion
  23.5 0.5 fusion.1
  23.9 0.6 copy-done.4
  24.6 0.0 reduce-scatter.5.cloned.1.call-start
  24.6 68.4 %all-gather.3.cloned.1.call-done = bf16[1024,2048]{1,0:T(8,128)(2,1)} async-done(((bf16[256,2048]{1,0:T(8,128)(2,1)}), bf16[1024,2048]{1,0:T(8,128)(2,1)}) %all-gather.3.cloned.1.call-update) | async-done | bytes 4194320 | tf_op jit(solution)/shard_map/all_gather | solution.py:47
  93.1 4.0 %fusion.15 = f32[1024,16]{0,1:T(8,128)} fusion(bf16[1024,2048]{1,0:T(8,128)(2,1)} %all-gather.3.cloned.1.call-done, bf16[16,2048]{1,0:T(8,128)(2,1)S(1)} %copy-done), kind=kOutput, calls=%fused_computation.34 | convolution fusion | flops 67108864 | bytes 4325376 | tf_op jit(solution)/shard_map/dot_general | solution.py:11
  97.1 0.0 reduce-scatter.3.cloned.1.call-start
  97.1 14.4 %fusion.14 = f32[1024,2048]{1,0:T(8,128)} fusion(bf16[1024,2048]{1,0:T(8,128)(2,1)} %all-gather.3.cloned.1.call-done, bf16[2048,2048]{1,0:T(8,128)(2,1)} %param.8), kind=kOutput, calls=%fused_computation.33 | convolution fusion | flops 8589934592 | bytes 20971520 | tf_op jit(solution)/shard_map/dot_general | solution.py:48
  111.6 0.1 fusion.17
  111.8 4.6 %fusion.16 = f32[16,2048]{1,0:T(8,128)S(1)} fusion(bf16[16,2048]{1,0:T(8,128)(2,1)S(1)} %copy-done, bf16[2048,2048]{1,0:T(8,128)(2,1)} %param.8), kind=kOutput, calls=%fused_computation.35 | convolution fusion | flops 134217728 | bytes 8585216 | tf_op jit(solution)/shard_map/dot_general | solution.py:42
  116.4 0.8 convolution_add_fusion.1
  117.3 14.9 %all-gather.5.cloned.1.call-done = f32[16,1024,16]{1,2,0:T(8,128)} async-done(((f32[1,1024,16]{1,2,0:T(8,128)}), f32[16,1024,16]{1,2,0:T(8,128)}) %all-gather.5.cloned.1.call-update) | async-done | bytes 1048592 | tf_op jit(solution)/shard_map/all_gather | solution.py:27
  132.3 1.3 reduce_sum.39
  133.5 20.3 %reduce-scatter.5.cloned.1.call-done = f32[256,16]{0,1:T(8,128)} async-done(((f32[1024,16]{0,1:T(8,128)}), f32[256,16]{0,1:T(8,128)}) %reduce-scatter.5.cloned.1.call-update) | async-done | bytes 16400 | tf_op jit(solution)/shard_map/reduce_scatter | solution.py:52
  153.8 1.8 fusion.2
  155.7 72.0 %reduce-scatter.3.cloned.1.call-done = f32[256,2048]{1,0:T(8,128)} async-done(((f32[1024,2048]{1,0:T(8,128)}), f32[256,2048]{1,0:T(8,128)}) %reduce-scatter.3.cloned.1.call-update) | async-done | bytes 2097168 | tf_op jit(solution)/shard_map/reduce_scatter | solution.py:51
  227.7 3.2 multiply_reduce_fusion.1
  230.9 12.8 %psum.36 = f32[2048]{0:T(1024)S(1)} all-reduce(f32[2048]{0:T(1024)S(1)} %get-tuple-element.4), channel_id=1, replica_groups=mesh['dp'=2,'row'=4,'col'=4] {'dp','row'}, use_global_device_ids=true, to_apply=%region_7.8 | all-reduce | flops 2048 | bytes 16384 | tf_op jit(solution)/shard_map/psum | solution.py:73
  243.7 0.6 fusion.7
  244.3 5.7 %fusion.4 = f32[16,2048]{1,0:T(8,128)S(1)} fusion(bf16[2048,2048]{1,0:T(8,128)(2,1)} %param.8, bf16[16,2048]{1,0:T(8,128)(2,1)S(1)} %copy-done.2, f32[2048]{0:T(1024)S(1)} %get-tuple-element.6), kind=kOutput, calls=%fused_computation.16 | convolution fusion | flops 134316032 | bytes 8593408 | tf_op jit(solution)/shard_map/dot_general | solution.py:11
  250.1 0.1 fusion.3
  250.2 0.2 fusion
  250.5 0.9 convolution_add_fusion.3
  251.4 10.3 %all-reduce.8.cloned.1.call-done = f32[16,2048]{1,0:T(8,128)} async-done(((f32[16,2048]{1,0:T(8,128)}), f32[16,2048]{1,0:T(8,128)}) %all-reduce.8.cloned.1.call-update) | async-done | bytes 131088 | tf_op jit(solution)/shard_map/psum | solution.py:54
  261.7 57.0 %all-reduce.6.cloned.1.call-done = f32[16,2048]{1,0:T(8,128)} async-done(((f32[16,2048]{1,0:T(8,128)}), f32[16,2048]{1,0:T(8,128)}) %all-reduce.6.cloned.1.call-update) | async-done | bytes 131088 | tf_op jit(solution)/shard_map/psum | solution.py:73
  318.7 1.6 multiply_add_fusion
  320.3 72.1 %all-reduce.4.cloned.1.call-done = f32[16,2048]{1,0:T(8,128)} async-done(((f32[16,2048]{1,0:T(8,128)}), f32[16,2048]{1,0:T(8,128)}) %all-reduce.4.cloned.1.call-update) | async-done | bytes 131088 | tf_op jit(solution)/shard_map/psum | solution.py:96
  392.4 1.6 copy.15
  (29 shorter events, 0.4 us)
Async XLA Ops:
  7.2 1.6 copy-start
  7.2 85.9 %all-gather.3.cloned.1.call-start = ((), (), s32[]{:S(2)}) async-start(), calls=%async_computation.2 | async-start | bytes 5242880 | tf_op jit(solution)/shard_map/all_gather | solution.py:47
  7.9 124.3 %all-gather.5.cloned.1.call-start = ((), (), s32[]{:S(2)}) async-start(), calls=%async_computation.5 | async-start | bytes 1114112 | tf_op jit(solution)/shard_map/all_gather | solution.py:27
  8.8 14.5 %copy-start.6 = (s32[1,8]{1,0:T(1,128)S(1)}, s32[1,8]{1,0:T(1,128)}, u32[]{:S(2)}) copy-start(s32[1,8]{1,0:T(1,128)} %param.13) | copy-start | bytes 100
  8.8 14.6 %copy-start.5 = (f32[2048]{0:T(1024)S(1)}, f32[2048]{0:T(1024)}, u32[]{:S(2)}) copy-start(f32[2048]{0:T(1024)} %param.11) | copy-start | bytes 24580
  8.8 14.6 %copy-start.2 = (bf16[16,2048]{1,0:T(8,128)(2,1)S(1)}, bf16[16,2048]{1,0:T(8,128)(2,1)}, u32[]{:S(2)}) copy-start(bf16[16,2048]{1,0:T(8,128)(2,1)} %param.10) | copy-start | bytes 196612
  8.8 14.6 %copy-start.3 = (bf16[256,2048]{1,0:T(8,128)(2,1)S(1)}, bf16[256,2048]{1,0:T(8,128)(2,1)}, u32[]{:S(2)}) copy-start(bf16[256,2048]{1,0:T(8,128)(2,1)} %param.12) | copy-start | bytes 3145732
  23.9 0.6 copy-start.4
  24.6 129.2 %reduce-scatter.5.cloned.1.call-start = ((), (), s32[]{:S(2)}) async-start(), calls=%async_computation.4 | async-start | bytes 81920 | tf_op jit(solution)/shard_map/reduce_scatter | solution.py:52
  97.1 130.6 %reduce-scatter.3.cloned.1.call-start = ((), (), s32[]{:S(2)}) async-start(), calls=%async_computation.3 | async-start | bytes 10485760 | tf_op jit(solution)/shard_map/reduce_scatter | solution.py:51
  111.6 150.1 %all-reduce.8.cloned.1.call-start = ((), (), s32[]{:S(2)}) async-start(), calls=%async_computation.8 | async-start | bytes 262144 | tf_op jit(solution)/shard_map/psum | solution.py:54
  117.2 201.4 %all-reduce.6.cloned.1.call-start = ((), (), s32[]{:S(2)}) async-start(), calls=%async_computation.7 | async-start | bytes 262144 | tf_op jit(solution)/shard_map/psum | solution.py:73
  155.6 236.7 %all-reduce.4.cloned.1.call-start = ((), (), s32[]{:S(2)}) async-start(), calls=%async_computation.6 | async-start | bytes 262144 | tf_op jit(solution)/shard_map/psum | solution.py:96
  244.3 6.1 %copy-start.1 = (bf16[256,2048]{1,0:T(8,128)(2,1)S(1)}, bf16[256,2048]{1,0:T(8,128)(2,1)}, u32[]{:S(2)}) copy-start(bf16[256,2048]{1,0:T(8,128)(2,1)} %param.7) | copy-start | bytes 3145732
Sparse Core Ops, SparseCore 0:
  9.6 83.4 all-gather.2
  95.8 36.3 all-gather.4
  135.2 18.5 reduce-scatter.4
  156.3 71.4 reduce-scatter.2
  229.9 31.7 all-reduce.7
  265.2 53.4 all-reduce.5
  322.6 69.7 all-reduce.3
